TPU v7x, 32 devices: a whole 2x2x4 slice. The times are simulated.
32 devices in a mesh: dev: 8 (over z, x), rep: 4 (over y, core).
Axes of the slice: x: 2, y: 2, z: 4, core: 2. Of those that a mesh axis runs over, the one named last changes fastest.
Arguments:
- emb_table: float32 [32768, 160], P('dev'), may hold values from -6 to 6
- feature_ids: int32 [4096, 4, 8], P(('dev', 'rep')), may hold values from 0 to 8191
- lengths: int32 [4096, 4], P(('dev', 'rep')), may hold values from 1 to 8
- cotangent: float32 [4096, 4, 160], P(('dev', 'rep')), may hold values from -6 to 6
Outputs:
- pooled: float32 [4096, 4, 160], P(('dev', 'rep'))
- row_grads: float32 [32768, 160], P(('dev', 'rep'))
All inputs are finite; a program needn't handle non-finite values.
Results may differ from a plain program's by a relative error of at most 0.00008.
Values sent between devices are 32-bit elements; how exact they have to be, the bound alone decides.
A program may use at most 128 MiB of HBM per device.

v0:
```python
import math

import jax
import jax.numpy as jnp
from jax import lax
from jax.sharding import PartitionSpec as P


def relative_ids(id_rows, base_row):
    live_count = jnp.sum((id_rows >= 0).astype(jnp.float32), axis=1)
    share = 1.0 / live_count
    shifted = jnp.where(id_rows >= 0, id_rows - base_row, -1)
    return (shifted, share)


def count_block(shifted, first_col, block_rows):
    columns = first_col + lax.broadcasted_iota(jnp.int32, (1, block_rows), 1)
    result = jnp.zeros((shifted.shape[0], block_rows), jnp.float32)
    for slot in range(shifted.shape[1]):
        result = result + (shifted[:, slot : slot + 1] == columns).astype(jnp.float32)
    return result


def pool_rows(shifted, share, table_rows):
    block_rows = math.gcd(table_rows.shape[0], 1024)
    block_count = table_rows.shape[0] // block_rows

    def add_block(block_index, partial_value):
        table_block = lax.dynamic_slice_in_dim(table_rows, block_index * block_rows, block_rows, 0)
        counts = count_block(shifted, block_index * block_rows, block_rows)
        return partial_value + jnp.dot(
            counts, table_block, precision=lax.Precision.HIGHEST, preferred_element_type=jnp.float32
        )

    start_pool = jnp.zeros((shifted.shape[0], table_rows.shape[1]), jnp.float32)
    summed = lax.fori_loop(0, block_count, add_block, start_pool)
    return summed * share[:, None]


def grad_rows(shifted, scaled, rows_dev):
    block_rows = math.gcd(rows_dev, 1024)
    block_count = rows_dev // block_rows

    def block_grad(block_index):
        counts = count_block(shifted, block_index * block_rows, block_rows)
        return jnp.dot(
            counts.T, scaled, precision=lax.Precision.HIGHEST, preferred_element_type=jnp.float32
        )

    blocks = lax.map(block_grad, jnp.arange(block_count, dtype=jnp.int32))
    return blocks.reshape(rows_dev, scaled.shape[1])


def body(emb_table, feature_ids, lengths, cotangent):
    dev_count = lax.axis_size("dev")
    rows_dev, emb_width = emb_table.shape
    examples, features, bag_len = feature_ids.shape
    owners_each = dev_count // features
    own_index = lax.axis_index("dev")
    own_feature = own_index // owners_each
    base_row = own_index % owners_each * rows_dev
    slot_index = lax.broadcasted_iota(jnp.int32, feature_ids.shape, 2)
    masked = jnp.where(slot_index < lengths[:, :, None], feature_ids, -1)
    all_ids = lax.all_gather(masked, "dev", axis=0, tiled=True)
    id_block = all_ids
    own_ids = lax.dynamic_index_in_dim(id_block, own_feature, 1, keepdims=False)
    shifted, share = relative_ids(own_ids, base_row)
    partial_value = pool_rows(shifted, share, emb_table)
    feature_pos = lax.broadcasted_iota(jnp.int32, (1, features, 1), 1)
    pooled = lax.psum_scatter(
        jnp.where(feature_pos == own_feature, partial_value[:, None, :], 0.0),
        "dev",
        scatter_dimension=0,
        tiled=True,
    )
    id_block = all_ids
    own_ids = lax.dynamic_index_in_dim(id_block, own_feature, 1, keepdims=False)
    shifted, share = relative_ids(own_ids, base_row)
    own_cot = lax.dynamic_index_in_dim(
        lax.all_gather(cotangent, "dev", axis=0, tiled=True), own_feature, 1, keepdims=False
    )
    group_grads = grad_rows(shifted, own_cot * share[:, None], rows_dev)
    row_grads = lax.psum_scatter(group_grads, "rep", scatter_dimension=0, tiled=True)
    return (pooled, row_grads)


def solution(mesh):
    return jax.shard_map(
        body,
        mesh=mesh,
        in_specs=(
            P("dev", None),
            P(("dev", "rep"), None, None),
            P(("dev", "rep"), None),
            P(("dev", "rep"), None, None),
        ),
        out_specs=(P(("dev", "rep"), None, None), P(("dev", "rep"), None)),
        check_vma=False,
    )
```

profile of v0, /device:TPU:0, one launch (start us, length us, event | category | flops | bytes accessed | tf_op | source)
XLA Modules:
  0.0 196.6 jit_solution(12251916925476041428)
XLA Ops:
  7.2 0.0 all-gather.2.cloned.1.call-start
  7.2 0.7 all-gather.2.cloned.1.call-update
  7.9 0.0 reduce-scatter.3.cloned.1.call-start
  8.0 0.7 fusion.74
  8.7 32.5 %all_gather.6 = s32[1024,4,8]{0,2,1:T(8,128)S(1)} all-gather(s32[128,4,8]{0,2,1:T(8,128)S(1)} %fusion.74), channel_id=1, replica_groups=mesh['dev'=8,'rep'=4] {'dev'}, dimensions={0}, use_global_device_ids=true | all-gather | bytes 147456 | tf_op jit(solution)/shard_map/all_gather | solution.py:64
  41.3 36.2 %while.25 = (s32[]{:T(128)}, f32[1024,160]{0,1:T(8,128)S(1)}, s32[1024,8]{0,1:T(8,128)S(1)}, f32[4096,160]{0,1:T(8,128)}, s32[]{:T(128)}, /*index=5*/s32[]{:T(128)}, s32[]{:T(128)}, s32[]{:T(128)}) while((s32[]{:T(128)}, f32[1024,160]{0,1:T(8,128)S(1)}, s32[1024,8]{0,1:T(8,128)S(1)}, f32[4096,160]{0,1:T(8,128)}, s32[]{:T(128)}, ...), condition=%wide.region_1.2_spmd.clone, body=%wide.region_0.1_spmd.clone.sunk | while | flops 2037711872 | bytes 2072733 | solution.py:36
  41.3 9.0 %fusion.93 = f32[1024,160]{0,1:T(8,128)S(1)} fusion(s32[1024]{0:T(1024)S(1)} %iota_add_fusion.5, s32[1024]{0:T(1024)S(1)} %bitcast.69, s32[1024]{0:T(1024)S(1)} %bitcast.70, s32[1024]{0:T(1024)S(1)} %bitcast.71, s32[1024]{0:T(1024)S(1)} %bitcast.72, s32[1024]{0:T(1024)S(1)} %bitcast.73, s32[1024]{0:T(1024)S(1)} %bitcast.74, s32[1024]{0:T(1024)S(1)} %bitcast.75, ...), kind=kOutput, calls=%fused_computation.68.clone.1 | convolution fusion | flops 2037710848 | bytes 2002949 | tf_op jit(solution)/shard_map/while/body/eval_jaxpr/dot_general | solution.py:31
  50.4 9.0 %fusion.93 = f32[1024,160]{0,1:T(8,128)S(1)} fusion(s32[1024]{0:T(1024)S(1)} %iota_add_fusion.5, s32[1024]{0:T(1024)S(1)} %bitcast.69, s32[1024]{0:T(1024)S(1)} %bitcast.70, s32[1024]{0:T(1024)S(1)} %bitcast.71, s32[1024]{0:T(1024)S(1)} %bitcast.72, s32[1024]{0:T(1024)S(1)} %bitcast.73, s32[1024]{0:T(1024)S(1)} %bitcast.74, s32[1024]{0:T(1024)S(1)} %bitcast.75, ...), kind=kOutput, calls=%fused_computation.68.clone.1 | convolution fusion | flops 2037710848 | bytes 2002949 | tf_op jit(solution)/shard_map/while/body/eval_jaxpr/dot_general | solution.py:31
  59.4 9.0 %fusion.93 = f32[1024,160]{0,1:T(8,128)S(1)} fusion(s32[1024]{0:T(1024)S(1)} %iota_add_fusion.5, s32[1024]{0:T(1024)S(1)} %bitcast.69, s32[1024]{0:T(1024)S(1)} %bitcast.70, s32[1024]{0:T(1024)S(1)} %bitcast.71, s32[1024]{0:T(1024)S(1)} %bitcast.72, s32[1024]{0:T(1024)S(1)} %bitcast.73, s32[1024]{0:T(1024)S(1)} %bitcast.74, s32[1024]{0:T(1024)S(1)} %bitcast.75, ...), kind=kOutput, calls=%fused_computation.68.clone.1 | convolution fusion | flops 2037710848 | bytes 2002949 | tf_op jit(solution)/shard_map/while/body/eval_jaxpr/dot_general | solution.py:31
  68.5 9.0 %fusion.93 = f32[1024,160]{0,1:T(8,128)S(1)} fusion(s32[1024]{0:T(1024)S(1)} %iota_add_fusion.5, s32[1024]{0:T(1024)S(1)} %bitcast.69, s32[1024]{0:T(1024)S(1)} %bitcast.70, s32[1024]{0:T(1024)S(1)} %bitcast.71, s32[1024]{0:T(1024)S(1)} %bitcast.72, s32[1024]{0:T(1024)S(1)} %bitcast.73, s32[1024]{0:T(1024)S(1)} %bitcast.74, s32[1024]{0:T(1024)S(1)} %bitcast.75, ...), kind=kOutput, calls=%fused_computation.68.clone.1 | convolution fusion | flops 2037710848 | bytes 2002949 | tf_op jit(solution)/shard_map/while/body/eval_jaxpr/dot_general | solution.py:31
  77.4 0.0 all-gather.2.cloned.1.call-done
  77.5 1.2 bitcast_multiply_fusion
  78.7 1.9 broadcast_select_fusion
  80.6 0.0 reduce-scatter.3.cloned.1.call-update
  80.6 0.2 reduce-scatter.5.cloned.1.call-start
  80.9 1.3 copy.6
  82.2 59.2 %while.24 = (s32[]{:T(128)}, f32[4,1024,160]{1,0,2:T(4,128)S(1)}, s32[1024,8]{0,1:T(8,128)S(1)}, s32[4]{0:T(128)S(1)}, f32[1024,160]{1,0:T(8,128)}, /*index=5*/s32[]{:T(128)}, s32[1]{0:T(128)}, s32[]{:T(128)}) while((s32[]{:T(128)}, f32[4,1024,160]{1,0,2:T(4,128)S(1)}, s32[1024,8]{0,1:T(8,128)S(1)}, s32[4]{0:T(128)S(1)}, ...), condition=%wide.region_5.6_spmd, body=%wide.region_4.5_spmd.sunk | while | flops 2037384192 | bytes 4038781 | solution.py:50
  82.2 0.6 dynamic_slice.31
  83.4 7.7 %fusion.89 = f32[1,1024,160]{1,2,0:T(8,128)S(1)} fusion(f32[1024,160]{1,0:T(8,128)} %get-tuple-element.300, s32[1024]{0:T(1024)S(1)} %iota_add_fusion.4, s32[1024]{0:T(1024)S(1)} %bitcast.77, s32[1024]{0:T(1024)S(1)} %bitcast.78, s32[1024]{0:T(1024)S(1)} %bitcast.79, s32[1024]{0:T(1024)S(1)} %bitcast.80, s32[1024]{0:T(1024)S(1)} %bitcast.81, ...), kind=kOutput, calls=%fused_computation.33.clone.1 | convolution fusion | flops 2037383168 | bytes 1347584 | tf_op jit(solution)/shard_map/while/body/eval_jaxpr/dot_general | solution.py:46
  91.1 0.7 copy.13
  91.8 5.2 %dynamic_update_slice.5 = f32[4,1024,160]{1,0,2:T(4,128)S(1)} dynamic-update-slice(f32[4,1024,160]{1,0,2:T(4,128)S(1)} %get-tuple-element.289, f32[1,1024,160]{1,0,2:T(1,128)S(1)} %copy.13, s32[]{:T(128)S(6)} %copy.23, s32[]{:T(128)} %constant.83.clone.1..sunk, s32[]{:T(128)} %constant.83.clone.1..sunk) | dynamic-update-slice | bytes 1310724 | tf_op jit(solution)/shard_map/while/body/jit(dynamic_update_index_in_dim)/dynamic_update_slice | solution.py:50
  97.0 0.6 dynamic_slice.31
  98.2 7.7 %fusion.89 = f32[1,1024,160]{1,2,0:T(8,128)S(1)} fusion(f32[1024,160]{1,0:T(8,128)} %get-tuple-element.300, s32[1024]{0:T(1024)S(1)} %iota_add_fusion.4, s32[1024]{0:T(1024)S(1)} %bitcast.77, s32[1024]{0:T(1024)S(1)} %bitcast.78, s32[1024]{0:T(1024)S(1)} %bitcast.79, s32[1024]{0:T(1024)S(1)} %bitcast.80, s32[1024]{0:T(1024)S(1)} %bitcast.81, ...), kind=kOutput, calls=%fused_computation.33.clone.1 | convolution fusion | flops 2037383168 | bytes 1347584 | tf_op jit(solution)/shard_map/while/body/eval_jaxpr/dot_general | solution.py:46
  105.9 0.7 copy.13
  106.6 5.2 %dynamic_update_slice.5 = f32[4,1024,160]{1,0,2:T(4,128)S(1)} dynamic-update-slice(f32[4,1024,160]{1,0,2:T(4,128)S(1)} %get-tuple-element.289, f32[1,1024,160]{1,0,2:T(1,128)S(1)} %copy.13, s32[]{:T(128)S(6)} %copy.23, s32[]{:T(128)} %constant.83.clone.1..sunk, s32[]{:T(128)} %constant.83.clone.1..sunk) | dynamic-update-slice | bytes 1310724 | tf_op jit(solution)/shard_map/while/body/jit(dynamic_update_index_in_dim)/dynamic_update_slice | solution.py:50
  111.8 0.6 dynamic_slice.31
  113.0 7.7 %fusion.89 = f32[1,1024,160]{1,2,0:T(8,128)S(1)} fusion(f32[1024,160]{1,0:T(8,128)} %get-tuple-element.300, s32[1024]{0:T(1024)S(1)} %iota_add_fusion.4, s32[1024]{0:T(1024)S(1)} %bitcast.77, s32[1024]{0:T(1024)S(1)} %bitcast.78, s32[1024]{0:T(1024)S(1)} %bitcast.79, s32[1024]{0:T(1024)S(1)} %bitcast.80, s32[1024]{0:T(1024)S(1)} %bitcast.81, ...), kind=kOutput, calls=%fused_computation.33.clone.1 | convolution fusion | flops 2037383168 | bytes 1347584 | tf_op jit(solution)/shard_map/while/body/eval_jaxpr/dot_general | solution.py:46
  120.7 0.7 copy.13
  121.4 5.2 %dynamic_update_slice.5 = f32[4,1024,160]{1,0,2:T(4,128)S(1)} dynamic-update-slice(f32[4,1024,160]{1,0,2:T(4,128)S(1)} %get-tuple-element.289, f32[1,1024,160]{1,0,2:T(1,128)S(1)} %copy.13, s32[]{:T(128)S(6)} %copy.23, s32[]{:T(128)} %constant.83.clone.1..sunk, s32[]{:T(128)} %constant.83.clone.1..sunk) | dynamic-update-slice | bytes 1310724 | tf_op jit(solution)/shard_map/while/body/jit(dynamic_update_index_in_dim)/dynamic_update_slice | solution.py:50
  126.6 0.6 dynamic_slice.31
  127.8 7.7 %fusion.89 = f32[1,1024,160]{1,2,0:T(8,128)S(1)} fusion(f32[1024,160]{1,0:T(8,128)} %get-tuple-element.300, s32[1024]{0:T(1024)S(1)} %iota_add_fusion.4, s32[1024]{0:T(1024)S(1)} %bitcast.77, s32[1024]{0:T(1024)S(1)} %bitcast.78, s32[1024]{0:T(1024)S(1)} %bitcast.79, s32[1024]{0:T(1024)S(1)} %bitcast.80, s32[1024]{0:T(1024)S(1)} %bitcast.81, ...), kind=kOutput, calls=%fused_computation.33.clone.1 | convolution fusion | flops 2037383168 | bytes 1347584 | tf_op jit(solution)/shard_map/while/body/eval_jaxpr/dot_general | solution.py:46
  135.5 0.7 copy.13
  136.2 5.2 %dynamic_update_slice.5 = f32[4,1024,160]{1,0,2:T(4,128)S(1)} dynamic-update-slice(f32[4,1024,160]{1,0,2:T(4,128)S(1)} %get-tuple-element.289, f32[1,1024,160]{1,0,2:T(1,128)S(1)} %copy.13, s32[]{:T(128)S(6)} %copy.23, s32[]{:T(128)} %constant.83.clone.1..sunk, s32[]{:T(128)} %constant.83.clone.1..sunk) | dynamic-update-slice | bytes 1310724 | tf_op jit(solution)/shard_map/while/body/jit(dynamic_update_index_in_dim)/dynamic_update_slice | solution.py:50
  141.4 3.7 %copy.11 = f32[20,8,4,1024]{3,1,2,0:T(8,128)} copy(f32[20,8,4,1024]{3,2,1,0:T(4,128)S(1)} %bitcast.67) | data formatting | bytes 5242880
  145.1 0.0 reduce-scatter.5.cloned.1.call-update
  145.1 8.2 %reduce-scatter.3.cloned.1.call-done = f32[128,4,160]{0,2,1:T(8,128)} async-done(((f32[1024,4,160]{0,2,1:T(8,128)}), f32[128,4,160]{0,2,1:T(8,128)}) %reduce-scatter.3.cloned.1.call-update) | async-done | bytes 327696 | tf_op jit(solution)/shard_map/reduce_scatter | solution.py:70
  153.4 36.7 %reduce-scatter.5.cloned.1.call-done = f32[1024,160]{0,1:T(8,128)} async-done(((f32[4096,160]{0,1:T(8,128)}), f32[1024,160]{0,1:T(8,128)}) %reduce-scatter.5.cloned.1.call-update) | async-done | bytes 655376 | tf_op jit(solution)/shard_map/reduce_scatter | solution.py:83
  (23 shorter events, 0.3 us)
Async XLA Ops:
  7.2 70.3 %all-gather.2.cloned.1.call-start = ((), (), s32[]{:S(2)}) async-start(), calls=%async_computation.3 | async-start | bytes 2949120 | tf_op jit(solution)/shard_map/all_gather | solution.py:80
  7.9 145.5 %reduce-scatter.3.cloned.1.call-start = ((), (), s32[]{:S(2)}) async-start(), calls=%async_computation.2 | async-start | bytes 2949120 | tf_op jit(solution)/shard_map/reduce_scatter | solution.py:70
  80.6 109.4 %reduce-scatter.5.cloned.1.call-start = ((), (), s32[]{:S(2)}) async-start(), calls=%async_computation.4 | async-start | bytes 3276800 | tf_op jit(solution)/shard_map/reduce_scatter | solution.py:83
Sparse Core Ops, SparseCore 0:
  10.0 59.5 all-gather.1
  80.8 72.5 reduce-scatter.2
  156.5 33.5 reduce-scatter.4
where the time goes:
time: 197 us
  matrix products  66.7 us (34%)
  waiting for transfers between devices  45.6 us (23%)
  blocking collectives  32.5 us (16%)
  local copies, waits for them, and re-layouts  30.9 us (16%)
  between operations  13.8 us (7%)
  other arithmetic  3.93 us (2%)
  loops' own time  2.7 us (1%)
    reduce_scatter x1, waiting for transfers between devices, body(): lax.psum_scatter(group_grads, 'rep', scatter_dimension=0, tiled=True)  36.7 us
    dot_general x4, matrix products, add_block(): jnp.dot(counts, table_block, precision=lax.Precision.HIGHEST, preferred_e...  35.9 us
    all_gather x1, blocking collectives, body(): all_ids = lax.all_gather(masked, 'dev', axis=0, tiled=True)  32.5 us
    dot_general x4, matrix products, block_grad(): jnp.dot(counts.T, scaled, precision=lax.Precision.HIGHEST, preferred_elem...  30.9 us
    dynamic_update_slice x8, local copies, waits for them, and re-layouts, grad_rows(): blocks = lax.map(block_grad, jnp.arange(block_count, dtype=jnp.int32))  23.3 us
    reduce_scatter x1, waiting for transfers between devices, body(): lax.psum_scatter(jnp.where(feature_pos == own_feature, partial_value[:, N...  8.24 us
  transfers between devices with their start and end apart: 3, of which 2 were waited for; matrix products, arithmetic and copies ran while one was open for 50% of the time, Pallas kernels for 0%

commit v1 on v0

v1 whole, which is shorter than its diff:
```python
import functools

import jax
import jax.numpy as jnp
from jax import lax
from jax.experimental import pallas as pl
from jax.experimental.pallas import tpu as pltpu
from jax.sharding import PartitionSpec as P

F32, BF16, I32 = jnp.float32, jnp.bfloat16, jnp.int32
ROW_TILE = 256


def split_bits(value):
    high = value.astype(BF16)
    low = (value - high.astype(F32)).astype(BF16)
    return high, low


def kernel(
    n, reps, table, ids, lens, cot, pooled, grads,
    ids_buf, cot_buf, counts, halves, part, part_in, scaled, total, landed,
    id_send, id_recv, cot_send, cot_recv, part_send, part_recv, row_send, row_recv,
):
    features, bag, each = ids.shape
    width, rows_dev = table.shape
    owners = n // features
    rows_out = rows_dev // reps
    levels = reps.bit_length() - 1
    me = lax.axis_index("dev")
    rep = lax.axis_index("rep")
    feature = me // owners
    base = me % owners * rows_dev

    def flipped(value, bit):
        return value + (1 - 2 * (value // (1 << bit) % 2)) * (1 << bit)

    barrier = pltpu.get_barrier_semaphore()
    for step in range(1, n):
        pl.semaphore_signal(
            barrier, inc=1, device_id={"dev": (me + step) % n},
            device_id_type=pl.DeviceIdType.MESH,
        )
    for level in range(levels):
        pl.semaphore_signal(
            barrier, inc=1, device_id={"rep": flipped(rep, level)},
            device_id_type=pl.DeviceIdType.MESH,
        )
    pl.semaphore_wait(barrier, n - 1 + levels)

    def id_copy(peer, source):
        return pltpu.make_async_remote_copy(
            src_ref=ids.at[peer // owners], dst_ref=ids_buf.at[source],
            send_sem=id_send.at[peer], recv_sem=id_recv.at[source],
            device_id={"dev": peer}, device_id_type=pl.DeviceIdType.MESH,
        )

    def cot_copy(peer, source):
        return pltpu.make_async_remote_copy(
            src_ref=cot.at[peer // owners], dst_ref=cot_buf.at[source],
            send_sem=cot_send.at[peer], recv_sem=cot_recv.at[source],
            device_id={"dev": peer}, device_id_type=pl.DeviceIdType.MESH,
        )

    def part_copy(peer, source):
        return pltpu.make_async_remote_copy(
            src_ref=part.at[peer], dst_ref=part_in.at[source],
            send_sem=part_send.at[peer], recv_sem=part_recv.at[source],
            device_id={"dev": peer}, device_id_type=pl.DeviceIdType.MESH,
        )

    for step in range(1, n):
        id_copy((me + step) % n, me).start()
    for step in range(1, n):
        cot_copy((me + step) % n, me).start()

    ids_buf[me] = ids[feature]
    cot_buf[me] = cot[feature]

    def split_table(tile, _):
        at = pl.ds(pl.multiple_of(tile * ROW_TILE, ROW_TILE), ROW_TILE)
        high, low = split_bits(table[:, at])
        halves[:width, at] = high
        halves[width:, at] = low
        return 0

    lax.fori_loop(0, rows_dev // ROW_TILE, split_table, 0)

    def pool_pair(pair, _):
        columns = pl.ds(pl.multiple_of(pair * 2 * each, 2 * each), 2 * each)
        blocks = []
        for half in range(2):
            step = pair * 2 + half
            source = (me - step + n) % n

            @pl.when(step > 0)
            def _():
                id_copy(source, source).wait_recv()

            blocks.append(ids_buf[source])
        slots = jnp.concatenate(blocks, axis=1) - base
        keys, times = [], []
        for j in range(bag):
            own = slots[j : j + 1]
            same = (slots == own).astype(I32)
            repeat = jnp.sum(same, axis=0, keepdims=True)
            keep = (own >= 0) & (own < rows_dev)
            if j:
                keep = keep & (jnp.sum(same[:j], axis=0, keepdims=True) == 0)
            keys.append(jnp.where(keep, own, -1))
            times.append(jnp.broadcast_to(repeat.astype(F32), (16, 2 * each)).astype(BF16))

        def count_tile(tile, _):
            start = pl.multiple_of(tile * ROW_TILE, ROW_TILE)
            wanted = []
            for j in range(bag):
                local = keys[j] - start
                local = jnp.where((local >= 0) & (local < ROW_TILE), local, -1)
                wanted.append(jnp.broadcast_to(local.astype(F32), (16, 2 * each)).astype(BF16))
            row = lax.broadcasted_iota(I32, (16, 2 * each), 0).astype(F32)
            for group in range(ROW_TILE // 16):
                here = (row + 16.0 * group).astype(BF16)
                found = jnp.zeros((16, 2 * each), BF16)
                for j in range(bag):
                    found = jnp.where(wanted[j] == here, times[j], found)
                counts[pl.ds(start + 16 * group, 16), columns] = found
            return 0

        lax.fori_loop(0, rows_dev // ROW_TILE, count_tile, 0)
        both = jnp.dot(halves[...], counts[:, columns], preferred_element_type=F32)
        pool = both[:width] + both[width:]
        for half in range(2):
            step = pair * 2 + half
            source = (me - step + n) % n
            mine = pool[:, half * each : (half + 1) * each]

            @pl.when(step == 0)
            def _():
                part_in[me] = mine

            @pl.when(step > 0)
            def _():
                part[source] = mine
                part_copy(source, me).start()

        return 0

    lax.fori_loop(0, n // 2, pool_pair, 0)

    def scale_step(step, _):
        source = (me - step + n) % n

        @pl.when(step > 0)
        def _():
            cot_copy(source, source).wait_recv()

        live = jnp.sum((ids_buf[source] >= 0).astype(F32), axis=0, keepdims=True)
        high, low = split_bits(cot_buf[source] * (1.0 / live))
        columns = pl.ds(pl.multiple_of(step * each, each), each)
        scaled[:width, columns] = high
        scaled[width:, columns] = low
        return 0

    lax.fori_loop(0, n, scale_step, 0)

    def grad_chunk(chunk, level, target):
        def grad_tile(tile, _):
            start = pl.multiple_of(tile * ROW_TILE, ROW_TILE)
            rows = pl.ds(pl.multiple_of(chunk * rows_out + start, ROW_TILE), ROW_TILE)
            both = lax.dot_general(
                scaled[...], counts[rows, :], (((1,), (1,)), ((), ())),
                preferred_element_type=F32,
            )
            target[:, pl.ds(start, ROW_TILE)] = both[:width] + both[width:]
            return 0

        lax.fori_loop(0, rows_out // ROW_TILE, grad_tile, 0)

    sent, first = [], [0]
    for level in range(levels):
        first.append(first[-1] + (1 << (levels - 1 - level)))

    def gather_in(chunk, level, target):
        for before in range(level):
            target[...] = target[...] + landed[first[before] + chunk // (1 << (before + 1))]

    def row_copy(slot, level):
        return pltpu.make_async_remote_copy(
            src_ref=total.at[slot], dst_ref=landed.at[slot],
            send_sem=row_send.at[slot], recv_sem=row_recv.at[slot],
            device_id={"rep": flipped(rep, level)}, device_id_type=pl.DeviceIdType.MESH,
        )

    def wait_level(level):
        for slot in range(first[level], first[level + 1]):
            row_copy(slot, level).wait_recv()

    for level in range(levels):
        span = 1 << (levels - 1 - level)
        chunks = []
        for far in reversed(range(span)):
            high = rep // (1 << (level + 1))
            for bit in range(levels):
                if far >> bit & 1:
                    high = flipped(high, bit)
            low = rep % (1 << level)
            other = 1 - rep // (1 << level) % 2
            chunk = (high * 2 + other) * (1 << level) + low
            chunks.append((first[level] + high, chunk))
        for slot, chunk in chunks:
            grad_chunk(chunk, level, total.at[slot])
            if level == 0:
                row_copy(slot, level).start()
        if level:
            wait_level(level - 1)
            for slot, chunk in chunks:
                gather_in(chunk, level, total.at[slot])
                row_copy(slot, level).start()
        sent.extend((slot, level) for slot, _ in chunks)
    grad_chunk(rep, levels, grads)

    for step in range(1, n):
        part_copy((me - step + n) % n, (me - step + n) % n).wait_recv()
    for feature_at in range(features):
        value = part_in[feature_at * owners]
        for owner in range(1, owners):
            value = value + part_in[feature_at * owners + owner]
        pooled[feature_at] = value * (1.0 / lens[feature_at : feature_at + 1].astype(F32))

    wait_level(levels - 1)
    gather_in(rep, levels, grads)
    for slot, level in sent:
        row_copy(slot, level).wait_send()
    for step in range(1, n):
        peer = (me + step) % n
        id_copy(peer, me).wait_send()
        cot_copy(peer, me).wait_send()
        part_copy(peer, me).wait_send()


def body(n, reps, emb_table, feature_ids, lengths, cotangent):
    rows_dev, width = emb_table.shape
    each, features, bag = feature_ids.shape
    ids = jnp.transpose(feature_ids, (1, 2, 0))
    lens = lengths.T
    slot_index = lax.broadcasted_iota(I32, ids.shape, 1)
    ids = jnp.where(slot_index < lens[:, None, :], ids, -(1 << 20))
    rows_out = rows_dev // reps
    sem = pltpu.SemaphoreType.DMA
    pooled, grads = pl.pallas_call(
        functools.partial(kernel, n, reps),
        out_shape=(
            jax.ShapeDtypeStruct((features, width, each), F32),
            jax.ShapeDtypeStruct((width, rows_out), F32),
        ),
        in_specs=[pl.BlockSpec(memory_space=pltpu.VMEM)] * 4,
        out_specs=[pl.BlockSpec(memory_space=pltpu.VMEM)] * 2,
        scratch_shapes=[
            pltpu.VMEM((n, bag, each), I32),
            pltpu.VMEM((n, width, each), F32),
            pltpu.VMEM((rows_dev, n * each), BF16),
            pltpu.VMEM((2 * width, rows_dev), BF16),
            pltpu.VMEM((n, width, each), F32),
            pltpu.VMEM((n, width, each), F32),
            pltpu.VMEM((2 * width, n * each), BF16),
            pltpu.VMEM((reps - 1, width, rows_out), F32),
            pltpu.VMEM((reps - 1, width, rows_out), F32),
            sem((n,)), sem((n,)), sem((n,)), sem((n,)), sem((n,)), sem((n,)),
            sem((reps - 1,)), sem((reps - 1,)),
        ],
        compiler_params=pltpu.CompilerParams(
            collective_id=0, has_side_effects=True, vmem_limit_bytes=60 * 1024 * 1024
        ),
    )(emb_table.T, ids, lens, jnp.transpose(cotangent, (1, 2, 0)))
    return jnp.transpose(pooled, (2, 0, 1)), grads.T


def solution(mesh):
    return jax.shard_map(
        functools.partial(body, mesh.shape["dev"], mesh.shape["rep"]),
        mesh=mesh,
        in_specs=(
            P("dev", None),
            P(("dev", "rep"), None, None),
            P(("dev", "rep"), None),
            P(("dev", "rep"), None, None),
        ),
        out_specs=(P(("dev", "rep"), None, None), P(("dev", "rep"), None)),
        check_vma=False,
    )
```

time: 197 us -> 58.4 us (0.30)
  the two profiles are of different devices: /device:TPU:0 before, /device:TPU:27 now
where the time goes in v1:
time: 58.4 us; the launch traced here: 58.1 us
  Pallas kernels  52.4 us (90%)
  local copies, waits for them, and re-layouts  3.7 us (6%)
  other arithmetic  1.33 us (2%)
  between operations  0.64 us (1%)
    pallas_call x1, Pallas kernels, body(): pl.pallas_call(functools.partial(kernel, n, reps), out_shape=(jax.ShapeDt...  52.4 us
    unnamed x2, local copies, waits for them, and re-layouts  3.7 us
    select_n x1, other arithmetic, body(): ids = jnp.where(slot_index < lens[:, None, :], ids, -(1 << 20))  1.33 us

profile of v1, /device:TPU:27, one launch (start us, length us, event | category | flops | bytes accessed | tf_op | source)
XLA Modules:
  0.0 58.1 jit_solution(15350287304001225210)
XLA Ops:
  0.6 1.3 %bitcast_select_fusion.ids = s32[4,8,128]{2,1,0:T(8,128)} fusion(s32[128,4,8]{0,2,1:T(8,128)} %param.5, s32[4,128]{1,0:T(4,128)} %bitcast.11), kind=kLoop, calls=%fused_computation | loop fusion | flops 8192 | bytes 34816 | tf_op jit(solution)/shard_map/jit(_where)/select_n | solution.py:247
  2.0 52.4 %shard_map.59 = (f32[4,160,128]{2,1,0:T(8,128)}, f32[160,1024]{1,0:T(8,128)}) custom-call(f32[160,4096]{1,0:T(8,128)} %bitcast.7, s32[4,8,128]{2,1,0:T(8,128)} %bitcast_select_fusion.ids, s32[4,128]{1,0:T(4,128)} %bitcast.12, f32[4,160,128]{2,1,0:T(8,128)} %bitcast.9), custom_call_target="tpu_custom_call" | custom-call | tf_op jit(solution)/shard_map/pallas_call | solution.py:250
  54.4 1.7 %copy.8 = f32[128,4,160]{0,2,1:T(8,128)} copy(f32[128,4,160]{0,2,1:T(8,128)} %bitcast.10) | data formatting | bytes 655360
  56.1 2.0 %copy.9 = f32[1024,160]{0,1:T(8,128)} copy(f32[1024,160]{0,1:T(8,128)} %bitcast.8) | data formatting | bytes 1310720

commit v2 on v1

v2 whole, which is shorter than its diff:
```python
import functools

import jax
import jax.numpy as jnp
from jax import lax
from jax.experimental import pallas as pl
from jax.experimental.pallas import tpu as pltpu
from jax.sharding import PartitionSpec as P

F32, BF16, I32 = jnp.float32, jnp.bfloat16, jnp.int32
ROW_TILE = 256


def split_bits(value):
    high = value.astype(BF16)
    low = (value - high.astype(F32)).astype(BF16)
    return high, low


def kernel(
    n, reps, table, ids, lens, cot, pooled, grads,
    ids_buf, cot_buf, counts, halves, part, part_in, pool_in, scaled, total, landed,
    id_send, id_recv, cot_send, cot_recv, pass_send,
    part_send, part_recv, pool_send, pool_recv, row_send, row_recv,
):
    features, bag, each = ids.shape
    width, rows_dev = table.shape
    owners = n // features
    rows_out = rows_dev // reps
    levels = reps.bit_length() - 1
    pairs = n // 2
    me = lax.axis_index("dev")
    rep = lax.axis_index("rep")
    feature = me // owners
    lane = me % owners
    base = lane * rows_dev

    def flipped(value, bit):
        return value + (1 - 2 * (value // (1 << bit) % 2)) * (1 << bit)

    def near(step):
        return (me + step) % n

    def beside(step):
        return feature * owners + (lane + step) % owners

    def across(step):
        return (feature + step) % features * owners + lane

    barrier = pltpu.get_barrier_semaphore()
    for step in range(1, n):
        pl.semaphore_signal(
            barrier, inc=1, device_id={"dev": near(step)}, device_id_type=pl.DeviceIdType.MESH
        )
    for level in range(levels):
        pl.semaphore_signal(
            barrier, inc=1, device_id={"rep": flipped(rep, level)},
            device_id_type=pl.DeviceIdType.MESH,
        )
    pl.semaphore_wait(barrier, n - 1 + levels)

    def remote(src, dst, send, recv, axis, to):
        return pltpu.make_async_remote_copy(
            src_ref=src, dst_ref=dst, send_sem=send, recv_sem=recv,
            device_id={axis: to}, device_id_type=pl.DeviceIdType.MESH,
        )

    def id_copy(peer, source):
        return remote(
            ids.at[peer // owners], ids_buf.at[source],
            id_send.at[peer], id_recv.at[source], "dev", peer,
        )

    def cot_copy(peer, source):
        return remote(
            cot.at[peer // owners], cot_buf.at[source],
            cot_send.at[peer], cot_recv.at[source], "dev", peer,
        )

    def pass_copy(source, step):
        return remote(
            cot_buf.at[source], cot_buf.at[source],
            pass_send.at[source // owners, step], cot_recv.at[source], "dev", beside(step),
        )

    def part_copy(source, slot):
        return remote(
            part.at[source], part_in.at[slot], part_send.at[source], part_recv.at[slot],
            "dev", feature * owners + source % owners,
        )

    def pool_copy(source, slot):
        return remote(
            part.at[source], pool_in.at[slot],
            pool_send.at[source // owners], pool_recv.at[slot], "dev", source,
        )

    for step in range(1, n):
        id_copy(near(step), me).start()
    for step in range(1, owners):
        cot_copy(beside(step), me).start()
    for step in range(1, features):
        cot_copy(across(step), me).start()

    ids_buf[me] = ids[feature]
    cot_buf[me] = cot[feature]

    def split_table(tile, _):
        at = pl.ds(pl.multiple_of(tile * ROW_TILE, ROW_TILE), ROW_TILE)
        high, low = split_bits(table[:, at])
        halves[:width, at] = high
        halves[width:, at] = low
        return 0

    lax.fori_loop(0, rows_dev // ROW_TILE, split_table, 0)

    def pass_on(step):
        source = across(features - step)
        cot_copy(source, source).wait_recv()
        for side in range(1, owners):
            pass_copy(source, side).start()

    def pair_columns(pair):
        return pl.ds(pl.multiple_of(pair * 2 * each, 2 * each), 2 * each)

    def count_pair(pair, _):
        columns = pair_columns(pair)
        blocks = []
        for half in range(2):
            step = pair * 2 + half
            source = (me - step + n) % n

            @pl.when(step > 0)
            def _():
                id_copy(source, source).wait_recv()

            blocks.append(ids_buf[source])
        slots = jnp.concatenate(blocks, axis=1) - base
        keys, times = [], []
        for j in range(bag):
            own = slots[j : j + 1]
            same = (slots == own).astype(I32)
            repeat = jnp.sum(same, axis=0, keepdims=True)
            keep = (own >= 0) & (own < rows_dev)
            if j:
                keep = keep & (jnp.sum(same[:j], axis=0, keepdims=True) == 0)
            keys.append(jnp.where(keep, own, -1))
            times.append(jnp.broadcast_to(repeat.astype(F32), (16, 2 * each)).astype(BF16))

        def count_tile(tile, _):
            start = pl.multiple_of(tile * ROW_TILE, ROW_TILE)
            wanted = []
            for j in range(bag):
                local = keys[j] - start
                local = jnp.where((local >= 0) & (local < ROW_TILE), local, -1)
                wanted.append(jnp.broadcast_to(local.astype(F32), (16, 2 * each)).astype(BF16))
            row = lax.broadcasted_iota(I32, (16, 2 * each), 0).astype(F32)
            for group in range(ROW_TILE // 16):
                here = (row + 16.0 * group).astype(BF16)
                found = jnp.zeros((16, 2 * each), BF16)
                for j in range(bag):
                    found = jnp.where(wanted[j] == here, times[j], found)
                counts[pl.ds(start + 16 * group, 16), columns] = found
            return 0

        lax.fori_loop(0, rows_dev // ROW_TILE, count_tile, 0)

        @pl.when((pair > 0) & (pair < features))
        def _():
            pass_on(pair)

        return 0

    lax.fori_loop(0, pairs, count_pair, 0)
    for step in range(pairs, features):
        pass_on(step)

    def scale_step(step, _):
        source = (me - step + n) % n

        @pl.when(source % owners != lane)
        def _():
            cot_copy(source, source).wait_recv()

        live = jnp.sum((ids_buf[source] >= 0).astype(F32), axis=0, keepdims=True)
        high, low = split_bits(cot_buf[source] * (1.0 / live))
        columns = pl.ds(pl.multiple_of(step * each, each), each)
        scaled[:width, columns] = high
        scaled[width:, columns] = low
        return 0

    lax.fori_loop(0, n, scale_step, 0)

    def grad_chunk(chunk, target):
        def grad_tile(tile, _):
            start = pl.multiple_of(tile * ROW_TILE, ROW_TILE)
            rows = pl.ds(pl.multiple_of(chunk * rows_out + start, ROW_TILE), ROW_TILE)
            both = lax.dot_general(
                scaled[...], counts[rows, :], (((1,), (1,)), ((), ())),
                preferred_element_type=F32,
            )
            target[:, pl.ds(start, ROW_TILE)] = both[:width] + both[width:]
            return 0

        lax.fori_loop(0, rows_out // ROW_TILE, grad_tile, 0)

    first = [0]
    for level in range(levels):
        first.append(first[-1] + (1 << (levels - 1 - level)))

    def row_copy(slot, level):
        return remote(
            total.at[slot], landed.at[slot], row_send.at[slot], row_recv.at[slot],
            "rep", flipped(rep, level),
        )

    def pool_pair(pair, _):
        both = jnp.dot(halves[...], counts[:, pair_columns(pair)], preferred_element_type=F32)
        pool = both[:width] + both[width:]
        for half in range(2):
            source = (me - (pair * 2 + half) + n) % n
            part[source] = pool[:, half * each : (half + 1) * each]

            @pl.when(source % owners != lane)
            def _():
                part_copy(source, source // owners * owners + lane).start()

        return 0

    def sum_parts(step):
        source = across(step)
        value = part[source]
        for side in range(1, owners):
            slot = source // owners * owners + (lane + side) % owners
            part_copy(source, slot).wait_recv()
            value = value + part_in[slot]
        if step:
            part[source] = value
            pool_copy(source, feature).start()
        else:
            pool_in[feature] = value

    sent = []
    for apart in reversed(range(reps)):
        if apart == reps // 2 - 1:
            lax.fori_loop(0, pairs, pool_pair, 0)
            for step in reversed(range(features)):
                sum_parts(step)
        level, chunk = 0, rep
        while level < levels and not apart >> level & 1:
            level += 1
        for bit in range(levels):
            if apart >> bit & 1:
                chunk = flipped(chunk, bit)
        target = grads
        if apart:
            slot = first[level] + chunk // (1 << (level + 1))
            target = total.at[slot]
        grad_chunk(chunk, target)
        for before in range(level):
            arrived = first[before] + chunk // (1 << (before + 1))
            if apart == 0 and before == levels - 1:
                for step in range(1, features):
                    pool_copy(across(step), across(step) // owners).wait_recv()
                for at in range(features):
                    pooled[at] = pool_in[at] * (1.0 / lens[at : at + 1].astype(F32))
            row_copy(arrived, before).wait_recv()
            target[...] = target[...] + landed[arrived]
        if apart:
            row_copy(slot, level).start()
            sent.append((slot, level))

    for slot, level in sent:
        row_copy(slot, level).wait_send()
    for step in range(1, n):
        id_copy(near(step), me).wait_send()
    for step in range(1, owners):
        cot_copy(beside(step), me).wait_send()
    for step in range(1, features):
        source = across(step)
        cot_copy(source, me).wait_send()
        pool_copy(source, feature).wait_send()
        for side in range(1, owners):
            pass_copy(source, side).wait_send()
    for at in range(features):
        for side in range(1, owners):
            source = at * owners + (lane + side) % owners
            part_copy(source, at * owners + lane).wait_send()


def body(n, reps, emb_table, feature_ids, lengths, cotangent):
    rows_dev, width = emb_table.shape
    each, features, bag = feature_ids.shape
    ids = jnp.transpose(feature_ids, (1, 2, 0))
    lens = lengths.T
    slot_index = lax.broadcasted_iota(I32, ids.shape, 1)
    ids = jnp.where(slot_index < lens[:, None, :], ids, -(1 << 20))
    rows_out = rows_dev // reps
    sem = pltpu.SemaphoreType.DMA
    pooled, grads = pl.pallas_call(
        functools.partial(kernel, n, reps),
        out_shape=(
            jax.ShapeDtypeStruct((features, width, each), F32),
            jax.ShapeDtypeStruct((width, rows_out), F32),
        ),
        in_specs=[pl.BlockSpec(memory_space=pltpu.VMEM)] * 4,
        out_specs=[pl.BlockSpec(memory_space=pltpu.VMEM)] * 2,
        scratch_shapes=[
            pltpu.VMEM((n, bag, each), I32),
            pltpu.VMEM((n, width, each), F32),
            pltpu.VMEM((rows_dev, n * each), BF16),
            pltpu.VMEM((2 * width, rows_dev), BF16),
            pltpu.VMEM((n, width, each), F32),
            pltpu.VMEM((n, width, each), F32),
            pltpu.VMEM((features, width, each), F32),
            pltpu.VMEM((2 * width, n * each), BF16),
            pltpu.VMEM((reps - 1, width, rows_out), F32),
            pltpu.VMEM((reps - 1, width, rows_out), F32),
            sem((n,)), sem((n,)), sem((n,)), sem((n,)), sem((features, n // features)),
            sem((n,)), sem((n,)), sem((features,)), sem((features,)),
            sem((reps - 1,)), sem((reps - 1,)),
        ],
        compiler_params=pltpu.CompilerParams(
            collective_id=0, has_side_effects=True, vmem_limit_bytes=60 * 1024 * 1024
        ),
    )(emb_table.T, ids, lens, jnp.transpose(cotangent, (1, 2, 0)))
    return jnp.transpose(pooled, (2, 0, 1)), grads.T


def solution(mesh):
    return jax.shard_map(
        functools.partial(body, mesh.shape["dev"], mesh.shape["rep"]),
        mesh=mesh,
        in_specs=(
            P("dev", None),
            P(("dev", "rep"), None, None),
            P(("dev", "rep"), None),
            P(("dev", "rep"), None, None),
        ),
        out_specs=(P(("dev", "rep"), None, None), P(("dev", "rep"), None)),
        check_vma=False,
    )
```

time: 58.4 us -> 49.5 us (0.85)
  the two profiles are of different devices: /device:TPU:27 before, /device:TPU:0 now
where the time goes in v2:
time: 49.5 us; the launch traced here: 49.2 us
  Pallas kernels  43.5 us (88%)
  local copies, waits for them, and re-layouts  3.7 us (7%)
  other arithmetic  1.33 us (3%)
  between operations  0.64 us (1%)
    pallas_call x1, Pallas kernels, body(): pl.pallas_call(functools.partial(kernel, n, reps), out_shape=(jax.ShapeDt...  43.5 us
    unnamed x2, local copies, waits for them, and re-layouts  3.7 us
    select_n x1, other arithmetic, body(): ids = jnp.where(slot_index < lens[:, None, :], ids, -(1 << 20))  1.33 us

profile of v2, /device:TPU:0, one launch (start us, length us, event | category | flops | bytes accessed | tf_op | source)
XLA Modules:
  0.0 49.2 jit_solution(3620633487644101031)
XLA Ops:
  0.6 1.3 %bitcast_select_fusion.ids = s32[4,8,128]{2,1,0:T(8,128)} fusion(s32[128,4,8]{0,2,1:T(8,128)} %param.5, s32[4,128]{1,0:T(4,128)} %bitcast.11), kind=kLoop, calls=%fused_computation | loop fusion | flops 8192 | bytes 34816 | tf_op jit(solution)/shard_map/jit(_where)/select_n | solution.py:297
  2.0 43.5 %shard_map.59 = (f32[4,160,128]{2,1,0:T(8,128)}, f32[160,1024]{1,0:T(8,128)}) custom-call(f32[160,4096]{1,0:T(8,128)} %bitcast.7, s32[4,8,128]{2,1,0:T(8,128)} %bitcast_select_fusion.ids, s32[4,128]{1,0:T(4,128)} %bitcast.12, f32[4,160,128]{2,1,0:T(8,128)} %bitcast.9), custom_call_target="tpu_custom_call" | custom-call | tf_op jit(solution)/shard_map/pallas_call | solution.py:300
  45.5 1.7 %copy.8 = f32[128,4,160]{0,2,1:T(8,128)} copy(f32[128,4,160]{0,2,1:T(8,128)} %bitcast.10) | data formatting | bytes 655360
  47.2 2.0 %copy.9 = f32[1024,160]{0,1:T(8,128)} copy(f32[1024,160]{0,1:T(8,128)} %bitcast.8) | data formatting | bytes 1310720

commit v3 on v2

--- a/solution.py
+++ b/solution.py
@@ -18,8 +18,8 @@
 
 
 def kernel(
-    n, reps, table, ids, lens, cot, pooled, grads,
-    ids_buf, cot_buf, counts, halves, part, part_in, pool_in, scaled, total, landed,
+    n, reps, table_in, ids_in, lens_in, cot_in, pool_in, grads, arrived_rows,
+    table, raw, lens, cot, ids, stage, ids_buf, cot_buf, counts, halves, part, part_in, scaled, total, landed,
     id_send, id_recv, cot_send, cot_recv, pass_send,
     part_send, part_recv, pool_send, pool_recv, row_send, row_recv,
 ):
@@ -57,6 +57,22 @@
             barrier, inc=1, device_id={"rep": flipped(rep, level)},
             device_id_type=pl.DeviceIdType.MESH,
         )
+    staged = [
+        pltpu.make_async_copy(src, dst, stage.at[at])
+        for at, (src, dst) in enumerate(
+            ((ids_in, raw), (lens_in, lens), (cot_in, cot), (table_in, table))
+        )
+    ]
+    for copy in staged:
+        copy.start()
+    staged[0].wait()
+    staged[1].wait()
+    slot_index = lax.broadcasted_iota(I32, (bag, each), 0)
+    for at in range(features):
+        ids[at] = jnp.where(slot_index < lens[at : at + 1], raw[at], -(1 << 20))
+    staged[2].wait()
+    ids_buf[me] = ids[feature]
+    cot_buf[me] = cot[feature]
     pl.semaphore_wait(barrier, n - 1 + levels)
 
     def remote(src, dst, send, recv, axis, to):
@@ -102,8 +118,7 @@
     for step in range(1, features):
         cot_copy(across(step), me).start()
 
-    ids_buf[me] = ids[feature]
-    cot_buf[me] = cot[feature]
+    staged[3].wait()
 
     def split_table(tile, _):
         at = pl.ds(pl.multiple_of(tile * ROW_TILE, ROW_TILE), ROW_TILE)
@@ -191,26 +206,24 @@
 
     lax.fori_loop(0, n, scale_step, 0)
 
-    def grad_chunk(chunk, target):
-        def grad_tile(tile, _):
-            start = pl.multiple_of(tile * ROW_TILE, ROW_TILE)
-            rows = pl.ds(pl.multiple_of(chunk * rows_out + start, ROW_TILE), ROW_TILE)
-            both = lax.dot_general(
-                scaled[...], counts[rows, :], (((1,), (1,)), ((), ())),
-                preferred_element_type=F32,
-            )
-            target[:, pl.ds(start, ROW_TILE)] = both[:width] + both[width:]
-            return 0
-
-        lax.fori_loop(0, rows_out // ROW_TILE, grad_tile, 0)
+    def grad_tile(chunk, tile):
+        start = pl.multiple_of(chunk * rows_out + tile * ROW_TILE, ROW_TILE)
+        both = lax.dot_general(
+            scaled[...], counts[pl.ds(start, ROW_TILE), :], (((1,), (1,)), ((), ())),
+            preferred_element_type=F32,
+        )
+        return both[:width] + both[width:]
 
     first = [0]
     for level in range(levels):
         first.append(first[-1] + (1 << (levels - 1 - level)))
 
-    def row_copy(slot, level):
-        return remote(
-            total.at[slot], landed.at[slot], row_send.at[slot], row_recv.at[slot],
+    tiles = rows_out // ROW_TILE
+
+    def row_copy(slot, level, tile):
+        return remote(
+            total.at[slot, tile], landed.at[slot, tile],
+            row_send.at[slot, tile], row_recv.at[slot, tile],
             "rep", flipped(rep, level),
         )
 
@@ -240,38 +253,52 @@
         else:
             pool_in[feature] = value
 
-    sent = []
-    for apart in reversed(range(reps)):
-        if apart == reps // 2 - 1:
-            lax.fori_loop(0, pairs, pool_pair, 0)
-            for step in reversed(range(features)):
-                sum_parts(step)
+    def place(apart):
         level, chunk = 0, rep
         while level < levels and not apart >> level & 1:
             level += 1
         for bit in range(levels):
             if apart >> bit & 1:
                 chunk = flipped(chunk, bit)
-        target = grads
+        return level, chunk, first[level] + chunk // (1 << (level + 1)) if apart else 0
+
+    def make_tile(apart, tile):
+        level, chunk, slot = place(apart)
+        value = grad_tile(chunk, tile)
+        for before in range(level):
+            if apart or before < levels - 1:
+                came = first[before] + chunk // (1 << (before + 1))
+                row_copy(came, before, tile).wait_recv()
+                value = value + landed[came, tile]
         if apart:
-            slot = first[level] + chunk // (1 << (level + 1))
-            target = total.at[slot]
-        grad_chunk(chunk, target)
-        for before in range(level):
-            arrived = first[before] + chunk // (1 << (before + 1))
-            if apart == 0 and before == levels - 1:
-                for step in range(1, features):
-                    pool_copy(across(step), across(step) // owners).wait_recv()
-                for at in range(features):
-                    pooled[at] = pool_in[at] * (1.0 / lens[at : at + 1].astype(F32))
-            row_copy(arrived, before).wait_recv()
-            target[...] = target[...] + landed[arrived]
-        if apart:
-            row_copy(slot, level).start()
-            sent.append((slot, level))
-
-    for slot, level in sent:
-        row_copy(slot, level).wait_send()
+            total[slot, tile] = value
+            row_copy(slot, level, tile).start()
+        else:
+            grads[:, tile * ROW_TILE : (tile + 1) * ROW_TILE] = value
+
+    far = reps // 2
+    for tile in range(tiles + 1):
+        for apart in reversed(range(far, reps)):
+            late = 1 - apart % 2
+            if 0 <= tile - late < tiles:
+                make_tile(apart, tile - late)
+    lax.fori_loop(0, pairs, pool_pair, 0)
+    for apart in reversed(range(far)):
+        for tile in range(tiles):
+            make_tile(apart, tile)
+    for step in reversed(range(features)):
+        sum_parts(step)
+    for step in range(1, features):
+        pool_copy(across(step), across(step) // owners).wait_recv()
+    came = first[levels - 1] + rep // (1 << levels)
+    for tile in range(tiles):
+        row_copy(came, levels - 1, tile).wait_recv()
+        arrived_rows[:, tile * ROW_TILE : (tile + 1) * ROW_TILE] = landed[came, tile]
+
+    for apart in range(1, reps):
+        level, _, slot = place(apart)
+        for tile in range(tiles):
+            row_copy(slot, level, tile).wait_send()
     for step in range(1, n):
         id_copy(near(step), me).wait_send()
     for step in range(1, owners):
@@ -288,42 +315,60 @@
             part_copy(source, at * owners + lane).wait_send()
 
 
+def finish(lens, pool, own, arrived, pooled, grads):
+    for at in range(pool.shape[0]):
+        pooled[at] = pool[at] * (1.0 / lens[at : at + 1].astype(F32))
+    grads[...] = own[...] + arrived[...]
+
+
 def body(n, reps, emb_table, feature_ids, lengths, cotangent):
     rows_dev, width = emb_table.shape
     each, features, bag = feature_ids.shape
-    ids = jnp.transpose(feature_ids, (1, 2, 0))
     lens = lengths.T
-    slot_index = lax.broadcasted_iota(I32, ids.shape, 1)
-    ids = jnp.where(slot_index < lens[:, None, :], ids, -(1 << 20))
     rows_out = rows_dev // reps
+    tiles = rows_out // ROW_TILE
     sem = pltpu.SemaphoreType.DMA
-    pooled, grads = pl.pallas_call(
+    vmem = pl.BlockSpec(memory_space=pltpu.VMEM)
+    pool_shape = jax.ShapeDtypeStruct((features, width, each), F32)
+    rows_shape = jax.ShapeDtypeStruct((width, rows_out), F32)
+    pool, own, arrived = pl.pallas_call(
         functools.partial(kernel, n, reps),
-        out_shape=(
-            jax.ShapeDtypeStruct((features, width, each), F32),
-            jax.ShapeDtypeStruct((width, rows_out), F32),
-        ),
-        in_specs=[pl.BlockSpec(memory_space=pltpu.VMEM)] * 4,
-        out_specs=[pl.BlockSpec(memory_space=pltpu.VMEM)] * 2,
+        out_shape=(pool_shape, rows_shape, rows_shape),
+        in_specs=[pl.BlockSpec(memory_space=pl.ANY)] * 4,
+        out_specs=[vmem] * 3,
         scratch_shapes=[
+            pltpu.VMEM((width, rows_dev), F32),
+            pltpu.VMEM((features, bag, each), I32),
+            pltpu.VMEM((features, each), I32),
+            pltpu.VMEM((features, width, each), F32),
+            pltpu.VMEM((features, bag, each), I32),
+            sem((4,)),
             pltpu.VMEM((n, bag, each), I32),
             pltpu.VMEM((n, width, each), F32),
             pltpu.VMEM((rows_dev, n * each), BF16),
             pltpu.VMEM((2 * width, rows_dev), BF16),
             pltpu.VMEM((n, width, each), F32),
             pltpu.VMEM((n, width, each), F32),
-            pltpu.VMEM((features, width, each), F32),
             pltpu.VMEM((2 * width, n * each), BF16),
-            pltpu.VMEM((reps - 1, width, rows_out), F32),
-            pltpu.VMEM((reps - 1, width, rows_out), F32),
+            pltpu.VMEM((reps - 1, tiles, width, ROW_TILE), F32),
+            pltpu.VMEM((reps - 1, tiles, width, ROW_TILE), F32),
             sem((n,)), sem((n,)), sem((n,)), sem((n,)), sem((features, n // features)),
             sem((n,)), sem((n,)), sem((features,)), sem((features,)),
-            sem((reps - 1,)), sem((reps - 1,)),
+            sem((reps - 1, tiles)), sem((reps - 1, tiles)),
         ],
         compiler_params=pltpu.CompilerParams(
             collective_id=0, has_side_effects=True, vmem_limit_bytes=60 * 1024 * 1024
         ),
-    )(emb_table.T, ids, lens, jnp.transpose(cotangent, (1, 2, 0)))
+    )(
+        emb_table.T, jnp.transpose(feature_ids, (1, 2, 0)), lens,
+        jnp.transpose(cotangent, (1, 2, 0)),
+    )
+    pooled, grads = pl.pallas_call(
+        finish,
+        out_shape=(pool_shape, rows_shape),
+        in_specs=[vmem] * 4,
+        out_specs=[vmem] * 2,
+    )(lens, pool, own, arrived)
     return jnp.transpose(pooled, (2, 0, 1)), grads.T
 
 

time: 49.5 us -> 47.6 us (0.962)
  local copies, waits for them, and re-layouts: 3.7 us -> 0 us
  Pallas kernels: 43.5 us -> 46.7 us
  other arithmetic: 1.33 us -> 0 us
    unnamed x2 -> x0, local copies, waits for them, and re-layouts: 3.7 us -> none
    pallas_call x1 -> x2, Pallas kernels: 43.5 us -> 46.7 us  [the longest x1 44.3 us: body(): pl.pallas_call(functools.partial(kernel, n, reps), out_shape=(pool_shape,...]
    select_n x1 -> x0, other arithmetic: 1.33 us -> none  [body(): ids = jnp.where(slot_index < lens[:, None, :], ids, -(1 << 20))]
where the time goes in v3:
time: 47.6 us; the launch traced here: 47.3 us
  Pallas kernels  46.7 us (98%)
  between operations  0.64 us (1%)
    pallas_call x1, Pallas kernels, body(): pl.pallas_call(functools.partial(kernel, n, reps), out_shape=(pool_shape,...  44.3 us
    pallas_call x1, Pallas kernels, body(): pl.pallas_call(finish, out_shape=(pool_shape, rows_shape), in_specs=[vmem...  2.39 us

profile of v3, /device:TPU:0, one launch (start us, length us, event | category | flops | bytes accessed | tf_op | source)
XLA Modules:
  0.0 47.3 jit_solution(5124607184260319204)
XLA Ops:
  0.6 44.3 %shard_map.59 = (f32[4,160,128]{2,1,0:T(8,128)}, f32[160,1024]{1,0:T(8,128)}, f32[160,1024]{1,0:T(8,128)}) custom-call(f32[160,4096]{1,0:T(8,128)} %bitcast.6, s32[4,8,128]{2,1,0:T(8,128)} %bitcast.8, s32[4,128]{1,0:T(4,128)} %bitcast.9, f32[4,160,128]{2,1,0:T(8,128)} %bitcast.7), custom_call_target="tpu_custom_call" | custom-call | tf_op jit(solution)/shard_map/pallas_call | solution.py:334
  45.0 2.4 %shard_map.60 = (f32[4,160,128]{2,1,0:T(8,128)}, f32[160,1024]{1,0:T(8,128)}) custom-call(s32[4,128]{1,0:T(4,128)} %bitcast.10, f32[4,160,128]{2,1,0:T(8,128)} %get-tuple-element.7.pool, f32[160,1024]{1,0:T(8,128)} %get-tuple-element.8.own, f32[160,1024]{1,0:T(8,128)} %get-tuple-element.9.arrived), custom_call_target="tpu_custom_call" | custom-call | tf_op jit(solution)/shard_map/pallas_call | solution.py:366

commit v4 on v3

--- a/solution.py
+++ b/solution.py
@@ -190,6 +190,21 @@
     for step in range(pairs, features):
         pass_on(step)
 
+    def pool_pair(pair, _):
+        both = jnp.dot(halves[...], counts[:, pair_columns(pair)], preferred_element_type=F32)
+        pool = both[:width] + both[width:]
+        for half in range(2):
+            source = (me - (pair * 2 + half) + n) % n
+            part[source] = pool[:, half * each : (half + 1) * each]
+
+            @pl.when(source % owners != lane)
+            def _():
+                part_copy(source, source // owners * owners + lane).start()
+
+        return 0
+
+    lax.fori_loop(0, pairs, pool_pair, 0)
+
     def scale_step(step, _):
         source = (me - step + n) % n
 
@@ -226,19 +241,6 @@
             row_send.at[slot, tile], row_recv.at[slot, tile],
             "rep", flipped(rep, level),
         )
-
-    def pool_pair(pair, _):
-        both = jnp.dot(halves[...], counts[:, pair_columns(pair)], preferred_element_type=F32)
-        pool = both[:width] + both[width:]
-        for half in range(2):
-            source = (me - (pair * 2 + half) + n) % n
-            part[source] = pool[:, half * each : (half + 1) * each]
-
-            @pl.when(source % owners != lane)
-            def _():
-                part_copy(source, source // owners * owners + lane).start()
-
-        return 0
 
     def sum_parts(step):
         source = across(step)
@@ -282,12 +284,12 @@
             late = 1 - apart % 2
             if 0 <= tile - late < tiles:
                 make_tile(apart, tile - late)
-    lax.fori_loop(0, pairs, pool_pair, 0)
     for apart in reversed(range(far)):
+        if apart == 0:
+            for step in reversed(range(features)):
+                sum_parts(step)
         for tile in range(tiles):
             make_tile(apart, tile)
-    for step in reversed(range(features)):
-        sum_parts(step)
     for step in range(1, features):
         pool_copy(across(step), across(step) // owners).wait_recv()
     came = first[levels - 1] + rep // (1 << levels)

time: 47.6 us -> 43.9 us (0.922)
  Pallas kernels: 46.7 us -> 43.1 us
    pallas_call x1, Pallas kernels: 44.3 us -> 40.7 us  [body(): pl.pallas_call(functools.partial(kernel, n, reps), out_shape=(pool_shape,...]
where the time goes in v4:
time: 43.9 us; the launch traced here: 43.7 us
  Pallas kernels  43.1 us (98%)
  between operations  0.64 us (1%)
    pallas_call x1, Pallas kernels, body(): pl.pallas_call(functools.partial(kernel, n, reps), out_shape=(pool_shape,...  40.7 us
    pallas_call x1, Pallas kernels, body(): pl.pallas_call(finish, out_shape=(pool_shape, rows_shape), in_specs=[vmem...  2.39 us

profile of v4, /device:TPU:0, one launch (start us, length us, event | category | flops | bytes accessed | tf_op | source)
XLA Modules:
  0.0 43.7 jit_solution(2796868616782467538)
XLA Ops:
  0.6 40.7 %shard_map.59 = (f32[4,160,128]{2,1,0:T(8,128)}, f32[160,1024]{1,0:T(8,128)}, f32[160,1024]{1,0:T(8,128)}) custom-call(f32[160,4096]{1,0:T(8,128)} %bitcast.6, s32[4,8,128]{2,1,0:T(8,128)} %bitcast.8, s32[4,128]{1,0:T(4,128)} %bitcast.9, f32[4,160,128]{2,1,0:T(8,128)} %bitcast.7), custom_call_target="tpu_custom_call" | custom-call | tf_op jit(solution)/shard_map/pallas_call | solution.py:336
  41.3 2.4 %shard_map.60 = (f32[4,160,128]{2,1,0:T(8,128)}, f32[160,1024]{1,0:T(8,128)}) custom-call(s32[4,128]{1,0:T(4,128)} %bitcast.10, f32[4,160,128]{2,1,0:T(8,128)} %get-tuple-element.7.pool, f32[160,1024]{1,0:T(8,128)} %get-tuple-element.8.own, f32[160,1024]{1,0:T(8,128)} %get-tuple-element.9.arrived), custom_call_target="tpu_custom_call" | custom-call | tf_op jit(solution)/shard_map/pallas_call | solution.py:368
